TPU v7x, 32 devices: a whole 2x2x4 slice. The times are simulated.
32 devices in a mesh: section: 4 (over y, x), dp: 4 (over z), tensor: 2 (over core).
Axes of the slice: x: 2, y: 2, z: 4, core: 2. Of those that a mesh axis runs over, the one named last changes fastest.
Arguments:
- activations: bfloat16 [512, 8192], P('dp', 'tensor'), may hold values from -6 to 6
- targets: bfloat16 [4, 512, 8192], P('section', 'dp', 'tensor'), may hold values from -12 to 12
- packed_floors: int32 [4, 2048, 8192], P('section', 'dp', 'tensor'), may hold values from 0 to 4095
- rounding: float32 [4, 8192, 8192], P('section', 'dp', 'tensor'), may hold values from -8 to 8
- scales: float32 [4, 8192], P('section', 'tensor'), may hold values from 0.001 to 0.006
- norm_gains: float32 [4, 8192], P('section'), may hold values from 0.5 to 1.5
Outputs:
- rounding_next: float32 [4, 8192, 8192], P('section', 'dp', 'tensor')
- block_outputs: bfloat16 [4, 512, 8192], P('section', 'dp', 'tensor')
- losses: float32 [4], P('section')
Inputs may be any that keep to these rules, and one draw needn't show every extreme that they name: `packed_floors`: each word holds four 3-bit codes in its lowest 12 bits, lowest bits first: code k of word r of a column is row 4 r + k; the floor is the code minus 4.
All inputs are finite; a program needn't handle non-finite values.
Results may differ from a plain program's by a relative error of at most 0.0045.
The roundings to bfloat16 on the way count: a program that leaves them out, or rounds other values in their place, can miss the bound.
Values may be sent and summed in bfloat16 or wider, within the bound.
A program may use at most 192 MiB of HBM per device.

v0:
```python
import jax
import jax.numpy as jnp
from jax import lax
from jax.sharding import PartitionSpec as P

MICRO = 4


norm_eps = 1e-06
grad_eps = 1e-06
reg_weight = 0.3
step_rate = 0.25
error_scale = 600.0


def passed_along(value, axis, steps):
    count = lax.axis_size(axis)
    leading, last = (max(0, -steps), min(count, count - steps))
    return lax.ppermute(value, axis, [(source, source + steps) for source in range(leading, last)])


def unpack(words):
    shifts = 3 * jnp.arange(4, dtype=jnp.int32)
    codes = jnp.right_shift(words[:, None, :], shifts[None, :, None]) & 7
    return codes.reshape(words.shape[0] * 4, words.shape[1]).astype(jnp.float32) - 4.0


def soft_round(values):
    sig = jax.nn.sigmoid(values)
    linear = 1.2 * sig - 0.1
    soft_part = jnp.clip(linear, 0.0, 1.0)
    soft_slope = jnp.where((linear > 0.0) & (linear < 1.0), 1.2 * sig * (1.0 - sig), 0.0)
    return (soft_part, soft_slope)


def normalize(features, gain_row):
    inputs = features.astype(jnp.float32)
    mean_sq = jnp.mean(inputs * inputs, axis=1, keepdims=True)
    return (inputs * lax.rsqrt(mean_sq + norm_eps) * gain_row[None, :]).astype(jnp.bfloat16)


def per_device(activations, targets, packed_floors, rounding, scales, norm_gains):
    section_index = lax.axis_index("section")
    section_count = lax.axis_size("section")
    dp_count = lax.axis_size("dp")
    tok_dev, width_local = activations.shape
    width_full = norm_gains.shape[1]
    token_total = tok_dev * dp_count
    floors = unpack(packed_floors[0])
    soft_part, soft_slope = soft_round(rounding[0])
    channel_scale = scales[0][None, :]
    soft_weight = (channel_scale * (floors + soft_part)).astype(jnp.bfloat16)
    gain_row = norm_gains[0]
    tok_micro = tok_dev // MICRO
    received = jnp.zeros((tok_micro, width_local), jnp.bfloat16)
    row_ticks = []
    output_ticks = []
    tick_count = MICRO + section_count - 1
    for tick_index in range(tick_count):
        fed = min(tick_index, MICRO - 1) * tok_micro
        block_input = jnp.where(section_index == 0, activations[fed : fed + tok_micro], received)
        whole_rows = lax.all_gather(block_input, "tensor", axis=1, tiled=True)
        normed = normalize(whole_rows, gain_row)
        swapped = lax.all_to_all(normed, "dp", split_axis=1, concat_axis=0, tiled=True)
        partial_value = jnp.dot(swapped, soft_weight, preferred_element_type=jnp.float32)
        branch = lax.psum_scatter(partial_value, "dp", scatter_dimension=0, tiled=True)
        block_result = (block_input.astype(jnp.float32) + branch).astype(jnp.bfloat16)
        row_ticks.append(swapped)
        output_ticks.append(block_result)
        if tick_index + 1 < tick_count:
            received = passed_along(block_result, "section", 1)
    stored_rows = lax.dynamic_slice_in_dim(jnp.stack(row_ticks), section_index, MICRO, axis=0)
    stored_rows = stored_rows.reshape(MICRO, dp_count, tok_micro, -1).transpose(1, 0, 2, 3)
    outputs_buf = lax.dynamic_slice_in_dim(
        jnp.concatenate(output_ticks), section_index * tok_micro, tok_dev, axis=0
    )
    residue = outputs_buf.astype(jnp.float32) - targets[0].astype(jnp.float32)
    delta = (error_scale / token_total**0.5 * residue).astype(jnp.bfloat16)
    delta_all = lax.all_gather(delta, "dp", axis=0, tiled=True)
    rows_all = stored_rows.reshape(dp_count * tok_dev, -1)
    grad_w = lax.dot_general(
        rows_all, delta_all, (((0,), (0,)), ((), ())), preferred_element_type=jnp.float32
    )
    polarity = 2.0 * soft_part - 1.0
    grad = soft_slope * (channel_scale * grad_w - 8.0 * reg_weight * polarity**3)
    recon_sum, penalty_sum, square_sum = lax.psum(
        (jnp.sum(residue * residue), jnp.sum(1.0 - polarity**4), jnp.sum(grad * grad)),
        ("dp", "tensor"),
    )
    mean_grad = square_sum / (width_full * width_full) + grad_eps
    rounding_next = rounding[0] - step_rate * grad * lax.rsqrt(mean_grad)
    loss_value = recon_sum / (token_total * width_full) + reg_weight * penalty_sum / (
        width_full * width_full
    )
    return (rounding_next[None], outputs_buf[None], loss_value.reshape(1))


def solution(mesh):
    placed = (
        P("dp", "tensor"),
        P("section", "dp", "tensor"),
        P("section", "dp", "tensor"),
        P("section", "dp", "tensor"),
        P("section", "tensor"),
        P("section", None),
    )
    return jax.shard_map(
        per_device,
        mesh=mesh,
        in_specs=placed,
        out_specs=(P("section", "dp", "tensor"), P("section", "dp", "tensor"), P("section")),
        check_vma=False,
    )
```

profile of v0, /device:TPU:7, one launch (start us, length us, event | category | flops | bytes accessed | tf_op | source)
XLA Modules:
  0.0 880.3 jit_solution(16472910666392996344)
XLA Ops:
  7.2 1.0 slice_select_fusion.2
  8.1 2.5 all_gather.24
  10.9 1.0 fusion.11
  11.8 0.8 copy.44
  12.7 4.6 all-to-all-start
  17.3 25.2 %add_clamp_fusion = f32[1,2048,4096]{2,1,0:T(8,128)} fusion(f32[1,2048,4096]{2,1,0:T(8,128)} %param.9), kind=kLoop, calls=%fused_computation.13 | loop fusion | flops 50331648 | bytes 67108864 | tf_op jit(solution)/shard_map/jit(clip)/min | solution.py:31
  42.5 37.4 %reshape.470 = f32[512,4,4096]{2,1,0:T(4,128)} reshape(f32[1,2048,4096]{2,1,0:T(8,128)} %add_clamp_fusion) | data formatting | bytes 67108864 | tf_op jit(solution)/shard_map/jit(clip)/min | solution.py:31
  79.9 20.5 %multiply_convert_fusion = bf16[512,4,4096]{2,1,0:T(4,128)(2,1)} fusion(f32[512,4,4096]{2,1,0:T(4,128)} %reshape.470, s32[4]{0:T(128)S(1)} %iota_multiply_fusion, s32[512,4096]{1,0:T(8,128)} %bitcast.110, f32[4096]{0:T(1024)S(1)} %bitcast.147), kind=kLoop, calls=%fused_computation.16 | loop fusion | flops 58720256 | bytes 58736656 | tf_op jit(solution)/shard_map/convert_element_type | solution.py:52
  100.5 23.7 %convert_element_type.171 = bf16[2048,4096]{1,0:T(8,128)(2,1)} reshape(bf16[512,4,4096]{2,1,0:T(4,128)(2,1)} %multiply_convert_fusion) | data formatting | bytes 33554432 | tf_op jit(solution)/shard_map/convert_element_type | solution.py:52
  124.2 9.5 %fusion.31 = f32[128,4096]{1,0:T(8,128)} fusion(bf16[128,2048]{1,0:T(8,128)(2,1)S(1)} %bitcast.112, bf16[2048,4096]{1,0:T(8,128)(2,1)} %convert_element_type.171), kind=kOutput, calls=%fused_computation.100 | convolution fusion | flops 2147483648 | bytes 19398656 | tf_op jit(solution)/shard_map/dot_general | solution.py:65
  133.8 44.7 %reduce-scatter.8.cloned.1.call-done = f32[32,4096]{1,0:T(8,128)} async-done(((f32[128,4096]{1,0:T(8,128)}), f32[32,4096]{1,0:T(8,128)}) %reduce-scatter.8.cloned.1.call-update) | async-done | bytes 524304 | tf_op jit(solution)/shard_map/reduce_scatter | solution.py:66
  178.5 1.8 constant_dynamic-update-slice_fusion.12
  180.3 1.3 collective-permute-start
  181.6 7.4 collective-permute-done
  189.0 3.7 all_gather.25
  193.2 16.8 %all_to_all.133 = bf16[32,4,2048]{2,0,1:T(8,128)(2,1)S(1)} all-to-all(bf16[32,4,2048]{2,0,1:T(8,128)(2,1)S(1)} %bitcast.134), channel_id=1, replica_groups=mesh['section'=4,'dp'=4,'tensor'=2] {'dp'}, dimensions={1} | all-to-all | bytes 1048576 | tf_op jit(solution)/shard_map/all_to_all | solution.py:64
  210.0 9.4 %fusion.32 = f32[128,4096]{1,0:T(8,128)} fusion(bf16[128,2048]{1,0:T(8,128)(2,1)S(1)} %bitcast.114, bf16[2048,4096]{1,0:T(8,128)(2,1)} %convert_element_type.171), kind=kOutput, calls=%fused_computation.101 | convolution fusion | flops 2147483648 | bytes 19398656 | tf_op jit(solution)/shard_map/dot_general | solution.py:65
  219.5 43.1 %reduce-scatter.10.cloned.1.call-done = f32[32,4096]{1,0:T(8,128)} async-done(((f32[128,4096]{1,0:T(8,128)}), f32[32,4096]{1,0:T(8,128)}) %reduce-scatter.10.cloned.1.call-update) | async-done | bytes 524304 | tf_op jit(solution)/shard_map/reduce_scatter | solution.py:66
  262.6 1.8 constant_dynamic-update-slice_fusion.11
  264.4 1.3 collective-permute-start.1
  265.7 7.4 collective-permute-done.1
  273.1 3.7 all_gather.26
  277.4 27.2 %all_to_all.134 = bf16[32,4,2048]{2,0,1:T(8,128)(2,1)S(1)} all-to-all(bf16[32,4,2048]{2,0,1:T(8,128)(2,1)S(1)} %bitcast.135), channel_id=1, replica_groups=mesh['section'=4,'dp'=4,'tensor'=2] {'dp'}, dimensions={1} | all-to-all | bytes 1048576 | tf_op jit(solution)/shard_map/all_to_all | solution.py:64
  304.5 9.4 %fusion.33 = f32[128,4096]{1,0:T(8,128)} fusion(bf16[128,2048]{1,0:T(8,128)(2,1)S(1)} %bitcast.116, bf16[2048,4096]{1,0:T(8,128)(2,1)} %convert_element_type.171), kind=kOutput, calls=%fused_computation.102 | convolution fusion | flops 2147483648 | bytes 19398656 | tf_op jit(solution)/shard_map/dot_general | solution.py:65
  314.1 43.1 %reduce-scatter.12.cloned.1.call-done = f32[32,4096]{1,0:T(8,128)} async-done(((f32[128,4096]{1,0:T(8,128)}), f32[32,4096]{1,0:T(8,128)}) %reduce-scatter.12.cloned.1.call-update) | async-done | bytes 524304 | tf_op jit(solution)/shard_map/reduce_scatter | solution.py:66
  357.1 1.8 constant_dynamic-update-slice_fusion.10
  358.9 1.3 collective-permute-start.2
  360.2 7.4 collective-permute-done.2
  367.6 3.7 all_gather.27
  371.9 16.8 %all_to_all.135 = bf16[32,4,2048]{2,0,1:T(8,128)(2,1)S(1)} all-to-all(bf16[32,4,2048]{2,0,1:T(8,128)(2,1)S(1)} %bitcast.136), channel_id=1, replica_groups=mesh['section'=4,'dp'=4,'tensor'=2] {'dp'}, dimensions={1} | all-to-all | bytes 1048576 | tf_op jit(solution)/shard_map/all_to_all | solution.py:64
  388.7 9.4 %fusion.34 = f32[128,4096]{1,0:T(8,128)} fusion(bf16[128,2048]{1,0:T(8,128)(2,1)S(1)} %bitcast.118, bf16[2048,4096]{1,0:T(8,128)(2,1)} %convert_element_type.171), kind=kOutput, calls=%fused_computation.103 | convolution fusion | flops 2147483648 | bytes 19398656 | tf_op jit(solution)/shard_map/dot_general | solution.py:65
  398.2 43.1 %reduce-scatter.14.cloned.1.call-done = f32[32,4096]{1,0:T(8,128)} async-done(((f32[128,4096]{1,0:T(8,128)}), f32[32,4096]{1,0:T(8,128)}) %reduce-scatter.14.cloned.1.call-update) | async-done | bytes 524304 | tf_op jit(solution)/shard_map/reduce_scatter | solution.py:66
  441.3 1.8 constant_dynamic-update-slice_fusion.9
  443.1 1.3 collective-permute-start.3
  444.4 7.4 collective-permute-done.3
  451.8 3.8 all_gather.28
  456.0 16.8 %all_to_all.136 = bf16[32,4,2048]{2,0,1:T(8,128)(2,1)S(1)} all-to-all(bf16[32,4,2048]{2,0,1:T(8,128)(2,1)S(1)} %bitcast.137), channel_id=1, replica_groups=mesh['section'=4,'dp'=4,'tensor'=2] {'dp'}, dimensions={1} | all-to-all | bytes 1048576 | tf_op jit(solution)/shard_map/all_to_all | solution.py:64
  472.8 9.4 %fusion.35 = f32[128,4096]{1,0:T(8,128)} fusion(bf16[128,2048]{1,0:T(8,128)(2,1)S(1)} %bitcast.120, bf16[2048,4096]{1,0:T(8,128)(2,1)} %convert_element_type.171), kind=kOutput, calls=%fused_computation.104 | convolution fusion | flops 2147483648 | bytes 19398656 | tf_op jit(solution)/shard_map/dot_general | solution.py:65
  482.3 43.1 %reduce-scatter.16.cloned.1.call-done = f32[32,4096]{1,0:T(8,128)} async-done(((f32[128,4096]{1,0:T(8,128)}), f32[32,4096]{1,0:T(8,128)}) %reduce-scatter.16.cloned.1.call-update) | async-done | bytes 524304 | tf_op jit(solution)/shard_map/reduce_scatter | solution.py:66
  525.4 1.8 constant_dynamic-update-slice_fusion.8
  527.2 1.3 collective-permute-start.4
  528.5 7.4 collective-permute-done.4
  535.9 1.0 broadcast_select_fusion.1
  536.9 3.8 all_gather.29
  541.1 16.8 %all_to_all.137 = bf16[32,4,2048]{2,0,1:T(8,128)(2,1)S(1)} all-to-all(bf16[32,4,2048]{2,0,1:T(8,128)(2,1)S(1)} %bitcast.138), channel_id=1, replica_groups=mesh['section'=4,'dp'=4,'tensor'=2] {'dp'}, dimensions={1} | all-to-all | bytes 1048576 | tf_op jit(solution)/shard_map/all_to_all | solution.py:64
  557.9 9.4 %fusion.36 = f32[128,4096]{1,0:T(8,128)} fusion(bf16[128,2048]{1,0:T(8,128)(2,1)S(1)} %bitcast.122, bf16[2048,4096]{1,0:T(8,128)(2,1)} %convert_element_type.171), kind=kOutput, calls=%fused_computation.105 | convolution fusion | flops 2147483648 | bytes 19398656 | tf_op jit(solution)/shard_map/dot_general | solution.py:65
  567.4 43.1 %reduce-scatter.18.cloned.1.call-done = f32[32,4096]{1,0:T(8,128)} async-done(((f32[128,4096]{1,0:T(8,128)}), f32[32,4096]{1,0:T(8,128)}) %reduce-scatter.18.cloned.1.call-update) | async-done | bytes 524304 | tf_op jit(solution)/shard_map/reduce_scatter | solution.py:66
  610.5 1.8 constant_dynamic-update-slice_fusion.7
  612.3 1.3 collective-permute-start.5
  613.6 7.4 collective-permute-done.5
  621.0 1.0 broadcast_select_fusion
  622.0 3.8 all_gather.30
  626.2 16.8 %all_to_all.138 = bf16[32,4,2048]{2,0,1:T(8,128)(2,1)S(1)} all-to-all(bf16[32,4,2048]{2,0,1:T(8,128)(2,1)S(1)} %bitcast.139), channel_id=1, replica_groups=mesh['section'=4,'dp'=4,'tensor'=2] {'dp'}, dimensions={1} | all-to-all | bytes 1048576 | tf_op jit(solution)/shard_map/all_to_all | solution.py:64
  643.0 0.8 copy-done
  643.8 9.5 %fusion.37 = f32[128,4096]{1,0:T(8,128)} fusion(bf16[128,2048]{1,0:T(8,128)(2,1)S(1)} %bitcast.124, bf16[2048,4096]{1,0:T(8,128)(2,1)} %convert_element_type.171), kind=kOutput, calls=%fused_computation.106 | convolution fusion | flops 2147483648 | bytes 19398656 | tf_op jit(solution)/shard_map/dot_general | solution.py:65
  653.6 42.9 %reduce-scatter.20.cloned.1.call-done = f32[32,4096]{1,0:T(8,128)} async-done(((f32[128,4096]{1,0:T(8,128)}), f32[32,4096]{1,0:T(8,128)}) %reduce-scatter.20.cloned.1.call-update) | async-done | bytes 524304 | tf_op jit(solution)/shard_map/reduce_scatter | solution.py:66
  696.5 1.8 fusion.30
  698.3 3.6 multiply_reduce_fusion.1
  701.9 19.6 %fusion.4 = f32[]{:T(128)} fusion(f32[1,2048,4096]{2,1,0:T(8,128)} %param.9), kind=kLoop, calls=%fused_computation.6 | loop fusion | flops 100663296 | bytes 33554436 | tf_op jit(solution)/shard_map/reduce_sum | solution.py:87
  722.2 1.1 dynamic-slice_bitcast_fusion
  723.3 59.0 %all-gather.2.cloned.1.call-done = bf16[512,4096]{1,0:T(8,128)(2,1)} async-done(((bf16[128,4096]{1,0:T(8,128)(2,1)}), bf16[512,4096]{1,0:T(8,128)(2,1)}) %all-gather.2.cloned.1.call-update) | async-done | bytes 4194320 | tf_op jit(solution)/shard_map/all_gather | solution.py:79
  782.2 39.9 %multiply_reduce_fusion = (f32[]{:T(128)}, f32[2048,4096]{1,0:T(8,128)}) fusion(bf16[512,2048]{1,0:T(8,128)(2,1)S(1)} %bitcast.126, bf16[512,4096]{1,0:T(8,128)(2,1)} %all-gather.2.cloned.1.call-done, f32[4096]{0:T(1024)S(1)} %bitcast.148, f32[1,2048,4096]{2,1,0:T(8,128)} %param.9), kind=kOutput, calls=%fused_computation.14 | convolution fusion | flops 8774483968 | bytes 73416704 | tf_op jit(solution)/shard_map/dot_general | solution.py:81
  822.1 14.5 %all-reduce = (f32[]{:T(128)}, f32[]{:T(128)}, f32[]{:T(128)}) all-reduce(f32[]{:T(128)} %get-tuple-element.20, f32[]{:T(128)} %get-tuple-element.18, f32[]{:T(128)} %fusion.4), channel_id=1, replica_groups=mesh['section'=4,'dp'=4,'tensor'=2] {'dp','tensor'}, use_global_device_ids=true, to_apply=%region_15.16 | all-reduce | flops 3 | bytes 24 | tf_op jit(solution)/shard_map/psum | solution.py:86
  838.5 33.4 %fusion.8 = f32[1,2048,4096]{2,1,0:T(8,128)} fusion(f32[1,2048,4096]{2,1,0:T(8,128)} %param.9, f32[2048,4096]{1,0:T(8,128)} %get-tuple-element.21, f32[]{:T(128)S(6)} %mul.311), kind=kLoop, calls=%fused_computation.12 | loop fusion | flops 16777216 | bytes 100663296 | tf_op jit(solution)/shard_map/broadcast_in_dim | solution.py:95
  (68 shorter events, 4.5 us)
Async XLA Ops:
  12.7 111.5 %all-to-all-start = ((bf16[32,4,2048]{2,0,1:T(8,128)(2,1)}), bf16[32,4,2048]{2,0,1:T(8,128)(2,1)S(1)}, u32[]{:S(2)}, u32[]{:S(2)}) async-start(bf16[32,4,2048]{2,0,1:T(8,128)(2,1)} %bitcast.109), calls=%async_computation | async-start | bytes 1048576 | tf_op jit(solution)/shard_map/all_to_all | solution.py:64
  17.3 161.2 %reduce-scatter.8.cloned.1.call-start = ((), (), s32[]{:S(2)}) async-start(), calls=%async_computation.14 | async-start | bytes 2621440 | tf_op jit(solution)/shard_map/reduce_scatter | solution.py:66
  42.5 37.4 %copy-start.5 = (f32[1,4096]{1,0:T(1,128)S(1)}, f32[1,4096]{1,0:T(1,128)}, u32[]{:S(2)}) copy-start(f32[1,4096]{1,0:T(1,128)} %param.10) | copy-start | bytes 49156
  124.1 54.3 %copy-start.2 = (bf16[128,4096]{1,0:T(8,128)(2,1)S(1)}, bf16[128,4096]{1,0:T(8,128)(2,1)}, u32[]{:S(2)}) copy-start(bf16[128,4096]{1,0:T(8,128)(2,1)} %param.6) | copy-start | bytes 3145732
  124.2 68.8 %copy-start.4 = (f32[1,8192]{1,0:T(1,128)S(1)}, f32[1,8192]{1,0:T(1,128)}, u32[]{:S(2)}) copy-start(f32[1,8192]{1,0:T(1,128)} %param.11) | copy-start | bytes 98308
  133.7 128.9 %reduce-scatter.10.cloned.1.call-start = ((), (), s32[]{:S(2)}) async-start(), calls=%async_computation.15 | async-start | bytes 2621440 | tf_op jit(solution)/shard_map/reduce_scatter | solution.py:66
  180.3 8.7 collective-permute-start
  219.5 137.6 %reduce-scatter.12.cloned.1.call-start = ((), (), s32[]{:S(2)}) async-start(), calls=%async_computation.16 | async-start | bytes 2621440 | tf_op jit(solution)/shard_map/reduce_scatter | solution.py:66
  264.4 8.7 collective-permute-start.1
  314.0 127.3 %reduce-scatter.14.cloned.1.call-start = ((), (), s32[]{:S(2)}) async-start(), calls=%async_computation.17 | async-start | bytes 2621440 | tf_op jit(solution)/shard_map/reduce_scatter | solution.py:66
  358.9 8.7 collective-permute-start.2
  398.1 127.3 %reduce-scatter.16.cloned.1.call-start = ((), (), s32[]{:S(2)}) async-start(), calls=%async_computation.18 | async-start | bytes 2621440 | tf_op jit(solution)/shard_map/reduce_scatter | solution.py:66
  443.1 8.7 collective-permute-start.3
  482.3 128.3 %reduce-scatter.18.cloned.1.call-start = ((), (), s32[]{:S(2)}) async-start(), calls=%async_computation.19 | async-start | bytes 2621440 | tf_op jit(solution)/shard_map/reduce_scatter | solution.py:66
  527.2 8.7 collective-permute-start.4
  567.4 129.1 %reduce-scatter.20.cloned.1.call-start = ((), (), s32[]{:S(2)}) async-start(), calls=%async_computation.20 | async-start | bytes 2621440 | tf_op jit(solution)/shard_map/reduce_scatter | solution.py:66
  612.3 8.7 collective-permute-start.5
  643.0 0.8 copy-start
  653.3 128.9 %all-gather.2.cloned.1.call-start = ((), (), s32[]{:S(2)}) async-start(), calls=%async_computation.21 | async-start | bytes 5242880 | tf_op jit(solution)/shard_map/all_gather | solution.py:79
  701.9 19.9 %copy-start.1 = (bf16[32,4,2048]{2,0,1:T(8,128)(2,1)S(1)}, bf16[32,4,2048]{2,0,1:T(8,128)(2,1)}, u32[]{:S(2)}) copy-start(bf16[32,4,2048]{2,0,1:T(8,128)(2,1)} %copy-done) | copy-start | bytes 1572868
  701.9 20.3 %copy-start.3 = (bf16[224,4096]{1,0:T(8,128)(2,1)S(1)}, bf16[224,4096]{1,0:T(8,128)(2,1)}, u32[]{:S(2)}) copy-start(bf16[224,4096]{1,0:T(8,128)(2,1)} %fusion.30) | copy-start | bytes 5505028
Sparse Core Ops, SparseCore 0:
  133.8 44.6 reduce-scatter.7
  219.6 42.9 reduce-scatter.9
  314.1 42.9 reduce-scatter.11
  398.2 42.9 reduce-scatter.13
  482.4 42.9 reduce-scatter.15
  567.5 42.9 reduce-scatter.17
  653.4 42.9 reduce-scatter.19
  702.0 80.1 all-gather.1
where the time goes:
time: 887 us; the launch traced here: 880 us
  waiting for transfers between devices  406 us (46%)
  blocking collectives  151 us (17%)
  other arithmetic  122 us (14%)
  matrix products  106 us (12%)
  local copies, waits for them, and re-layouts  64.7 us (7%)
  between operations  17.9 us (2%)
  starting transfers between devices  12.7 us (1%)
    reduce_scatter x7, waiting for transfers between devices, per_device(): lax.psum_scatter(partial_value, 'dp', scatter_dimension=0, tiled=True)  303 us
    all_to_all x6, blocking collectives, per_device(): lax.all_to_all(normed, 'dp', split_axis=1, concat_axis=0, tiled=True)  111 us
    dot_general x7, matrix products, per_device(): jnp.dot(swapped, soft_weight, preferred_element_type=jnp.float32)  66.1 us
    all_gather x1, waiting for transfers between devices, per_device(): delta_all = lax.all_gather(delta, 'dp', axis=0, tiled=True)  59 us
    ppermute x6, waiting for transfers between devices, passed_along(): lax.ppermute(value, axis, [(source, source + steps) for source in range(l...  44.3 us
    dot_general x1, matrix products, per_device(): lax.dot_general(rows_all, delta_all, (((0,), (0,)), ((), ())), preferred_...  39.9 us
    min x1, local copies, waits for them, and re-layouts, soft_round(): soft_part = jnp.clip(linear, 0.0, 1.0)  37.4 us
    broadcast_in_dim x1, other arithmetic, per_device(): return (rounding_next[None], outputs_buf[None], loss_value.reshape(1))  33.4 us
  transfers between devices with their start and end apart: 15, of which 14 were waited for; matrix products, arithmetic and copies ran while one was open for 15% of the time, Pallas kernels for 0%

commit v1 on v0

v1 whole, which is shorter than its diff:
```python
import functools
import jax
import jax.numpy as jnp
from jax import lax
from jax.experimental import pallas as pl
from jax.experimental.pallas import tpu as pltpu
from jax.sharding import PartitionSpec as P

MICRO = 4
SPLIT = 4


norm_eps = 1e-06
grad_eps = 1e-06
reg_weight = 0.3
step_rate = 0.25
error_scale = 600.0

VMEM_ALL = 62 * 1024 * 1024


def tile_of(size, most):
    while size % most:
        most //= 2
    return most


def weight_kernel(packed_ref, rounding_ref, scale_ref, weight_ref):
    rows, cols = rounding_ref.shape
    strip_c = tile_of(cols, 512)
    strip_r = 32

    @pl.loop(0, cols // strip_c)
    def _(cb):
        col = pl.ds(pl.multiple_of(cb * strip_c, strip_c), strip_c)
        scale = scale_ref[:, col]
        shift = 3 * (lax.broadcasted_iota(jnp.int32, (strip_r, strip_c), 0) & 3)

        @pl.loop(0, rows // strip_r)
        def _(rb):
            row = pl.ds(pl.multiple_of(rb * strip_r, strip_r), strip_r)
            word = pl.ds(pl.multiple_of(rb * (strip_r // 4), strip_r // 4), strip_r // 4)
            words = jnp.repeat(packed_ref[word, col], 4, axis=0)
            codes = (jnp.right_shift(words, shift) & 7).astype(jnp.float32)
            half = jnp.tanh(0.5 * rounding_ref[row, col])
            soft = jnp.clip(0.6 * half + 0.5, 0.0, 1.0)
            weight_ref[row, col] = (scale * ((codes - 4.0) + soft)).astype(jnp.bfloat16)


def make_weight(packed, rounding, scale_row):
    rows, cols = rounding.shape
    tr, tc = tile_of(rows, 256), tile_of(cols, 2048)
    return pl.pallas_call(
        weight_kernel,
        out_shape=jax.ShapeDtypeStruct((rows, cols), jnp.bfloat16),
        grid=(cols // tc, rows // tr),
        in_specs=[
            pl.BlockSpec((tr // 4, tc), lambda j, i: (i, j)),
            pl.BlockSpec((tr, tc), lambda j, i: (i, j)),
            pl.BlockSpec((1, tc), lambda j, i: (0, j)),
        ],
        out_specs=pl.BlockSpec((tr, tc), lambda j, i: (i, j)),
        compiler_params=pltpu.CompilerParams(dimension_semantics=("arbitrary", "arbitrary")),
        cost_estimate=pl.CostEstimate(
            flops=20 * rows * cols, transcendentals=rows * cols, bytes_accessed=7 * rows * cols
        ),
    )(packed, rounding, scale_row)


def grad_kernel(rows_ref, delta_ref, rounding_ref, scale_ref, grad_ref, sums_ref, product):
    trow, tcol = rounding_ref.shape
    strip_c = tile_of(tcol, 512)
    strip_r = 16
    first = (pl.program_id(0) == 0) & (pl.program_id(1) == 0)

    @pl.when(first)
    def _():
        sums_ref[...] = jnp.zeros_like(sums_ref)

    product[...] = lax.dot_general(
        rows_ref[...], delta_ref[...], (((0,), (0,)), ((), ())), preferred_element_type=jnp.float32
    )

    @pl.loop(0, tcol // strip_c)
    def _(cb):
        col = pl.ds(pl.multiple_of(cb * strip_c, strip_c), strip_c)
        scale = scale_ref[:, col]

        def strip(rb, sums):
            row = pl.ds(pl.multiple_of(rb * strip_r, strip_r), strip_r)
            full = 1.2 * jnp.tanh(0.5 * rounding_ref[row, col])
            inside = jnp.abs(full) < 1.0
            polarity = jnp.clip(full, -1.0, 1.0)
            square = polarity * polarity
            slope = jnp.where(inside, 0.3 - (0.3 / 1.44) * square, 0.0)
            grad = slope * (scale * product[row, col] - (8.0 * reg_weight) * (square * polarity))
            grad_ref[row, col] = grad.astype(grad_ref.dtype)
            fold = lambda v: v.reshape(strip_r // 8, 8, strip_c).sum(axis=0)
            return sums[0] + fold(grad * grad), sums[1] + fold(1.0 - square * square)

        zero = jnp.zeros((8, strip_c), jnp.float32)
        grads, pens = lax.fori_loop(0, trow // strip_r, strip, (zero, zero))
        lanes = lambda v: sum(v[:, k : k + 128] for k in range(0, strip_c, 128))
        sums_ref[0] += lanes(grads)
        sums_ref[1] += lanes(pens)


def make_grad(rows_all, delta_all, rounding, scale_row):
    tokens, rows = rows_all.shape
    cols = delta_all.shape[1]
    tr, tc = tile_of(rows, 256), tile_of(cols, 2048)
    return pl.pallas_call(
        grad_kernel,
        out_shape=(
            jax.ShapeDtypeStruct((rows, cols), jnp.bfloat16),
            jax.ShapeDtypeStruct((2, 8, 128), jnp.float32),
        ),
        grid=(cols // tc, rows // tr),
        in_specs=[
            pl.BlockSpec((tokens, tr), lambda j, i: (0, i)),
            pl.BlockSpec((tokens, tc), lambda j, i: (0, j)),
            pl.BlockSpec((tr, tc), lambda j, i: (i, j)),
            pl.BlockSpec((1, tc), lambda j, i: (0, j)),
        ],
        out_specs=(
            pl.BlockSpec((tr, tc), lambda j, i: (i, j)),
            pl.BlockSpec((2, 8, 128), lambda j, i: (0, 0, 0)),
        ),
        scratch_shapes=[pltpu.VMEM((tr, tc), jnp.float32)],
        compiler_params=pltpu.CompilerParams(dimension_semantics=("arbitrary", "arbitrary")),
        cost_estimate=pl.CostEstimate(
            flops=2 * tokens * rows * cols, transcendentals=rows * cols, bytes_accessed=6 * rows * cols
        ),
    )(rows_all, delta_all, rounding, scale_row)


def chain_kernel(
    act_ref, target_ref, weight_hbm, gain_ref, gain_next_ref,
    out_ref, residue_ref, rows_hbm, delta_hbm,
    weight, rows, part, own, landed, carried, normed, normed0, stat, delta,
    w_sem, row_sem, relay_sem, part_send, part_recv, carry_sem, carry_recv,
    norm_send, norm0_send, stat_send, stat_recv, delta_send, delta_recv, store_sem,
):
    section, z, t = (lax.axis_index(name) for name in ("section", "dp", "tensor"))
    sections, dp, nt = (lax.axis_size(name) for name in ("section", "dp", "tensor"))
    micro, _, tok, depth = rows.shape
    cols = out_ref.shape[1]
    pieces = cols // depth
    wide = cols // SPLIT
    model = depth * dp
    first = section == 0
    inner = section < sections - 1

    def remote(src, dst, send, recv, s, d, c):
        return pltpu.make_async_remote_copy(
            src_ref=src, dst_ref=dst, send_sem=send, recv_sem=recv,
            device_id={"section": s, "dp": d, "tensor": c}, device_id_type=pl.DeviceIdType.MESH,
        )

    def arrived(dst, recv):
        remote(dst, dst, recv, recv, section, z, t).wait_recv()

    def left(src, send):
        remote(src, src, send, send, section, z, t).wait_send()

    def columns(q):
        return pl.ds(q * wide, wide)

    def weight_copy(q):
        return pltpu.make_async_copy(
            weight_hbm.at[:, columns(q)], weight.at[:, columns(q)], w_sem.at[q]
        )

    for q in range(SPLIT):
        weight_copy(q).start()

    def token_rows(m):
        return pl.ds(m * tok, tok)

    def stat_start(kind, m, total):
        stat[kind, m, t] = jnp.broadcast_to(total, (tok, 128))
        for k in range(1, nt):
            remote(
                stat.at[kind, m, t], stat.at[kind, m, t], stat_send.at[kind, m, k], stat_recv.at[kind, m, t],
                section, z, lax.rem(t + k, nt),
            ).start()

    def inverse(kind, m):
        for k in range(1, nt):
            other = lax.rem(t + k, nt)
            arrived(stat.at[kind, m, other], stat_recv.at[kind, m, other])
        total = stat[kind, m, 0][:, :1]
        for k in range(1, nt):
            total = total + stat[kind, m, k][:, :1]
        return lax.rsqrt(total / model + norm_eps)

    entry = lax.rem(z, nt)

    def at_home(c):
        return first & (t * pieces + c == z) & (entry == t)

    def norm_copy(m, c, initial):
        buf, sem = (normed0, norm0_send) if initial else (normed, norm_send)
        return remote(
            buf.at[m, c], rows.at[m, z], sem.at[m, c], row_sem.at[m, z],
            section if initial else section + 1, t * pieces + c, entry,
        )

    def spread(m, src, gain, initial):
        inv = inverse(0 if initial else 1, m)
        buf = normed0 if initial else normed
        for c in range(pieces):
            cut = pl.ds(c * depth, depth)
            value = (src[token_rows(m), cut].astype(jnp.float32) * inv * gain[:, cut]).astype(jnp.bfloat16)
            buf[m, c] = value
            if initial:

                @pl.when(at_home(c))
                def _():
                    rows[m, z] = value

                @pl.when(jnp.logical_not(at_home(c)))
                def _():
                    norm_copy(m, c, True).start()
            else:
                norm_copy(m, c, False).start()

    @pl.when(first)
    def _():
        for m in range(micro):
            value = act_ref[token_rows(m), :]
            carried[m] = value
            value = value.astype(jnp.float32)
            stat_start(0, m, jnp.sum(value * value, axis=1, keepdims=True))
        for m in range(micro):
            spread(m, act_ref, gain_ref, True)

    home_piece = lax.rem(z, pieces)
    is_sender = t == z // pieces

    def relay(m, o, k):
        return remote(
            rows.at[m, o], rows.at[m, o], relay_sem.at[m, o, k], row_sem.at[m, o],
            section, z, lax.rem(t + k, nt),
        )

    def receive_rows(m):
        for o in range(dp):
            local = first & (z == o) & is_sender

            @pl.when((t == o % nt) & jnp.logical_not(local))
            def _():
                arrived(rows.at[m, o], row_sem.at[m, o])

            @pl.when(t == o % nt)
            def _():
                for k in range(1, nt):
                    relay(m, o, k).start()

        for o in range(dp):

            @pl.when(t != o % nt)
            def _():
                arrived(rows.at[m, o], row_sem.at[m, o])

    def rows_store(m):
        return pltpu.make_async_copy(rows.at[m], rows_hbm.at[m], store_sem.at[m])

    def part_copy(m, q, k):
        to = lax.rem(z + k, dp)
        return remote(
            part.at[m, to, :, columns(q)], landed.at[m, z, :, columns(q)],
            part_send.at[m, q, k], part_recv.at[m, q, z], section, to, t,
        )

    def multiply(m):
        step = tile_of(wide, 256)
        for q in range(SPLIT):
            if m == 0:
                weight_copy(q).wait()

            @pl.loop(0, wide // step)
            def _(b):
                cut = pl.ds(pl.multiple_of(q * wide + b * step, step), step)
                value = jnp.dot(
                    rows[m].reshape(dp * tok, depth), weight[:, cut], preferred_element_type=jnp.float32
                )
                own[:, :, cut] = value.reshape(dp, tok, step)
                part[m, :, :, cut] = value.reshape(dp, tok, step).astype(jnp.bfloat16)

            for k in range(1, dp):
                part_copy(m, q, k).start()

    def hand_on(m, origin, way):
        return remote(
            delta.at[m, origin], delta.at[m, origin], delta_send.at[m, origin, way], delta_recv.at[m, origin],
            section, z + (1 if way else -1), t,
        )

    def gather_step(m, hop):
        for way in (0, 1):
            origin = z - hop if way else z + hop
            exists = (origin >= 0) & (origin < dp)
            onward = exists & ((z + 1 < dp) if way else (z >= 1))
            if hop:

                @pl.when(exists)
                def _():
                    arrived(delta.at[m, origin], delta_recv.at[m, origin])

            @pl.when(onward)
            def _():
                hand_on(m, origin, way).start()

    def finish(m):
        total = jnp.zeros((tok, 1), jnp.float32)
        squares = jnp.zeros((tok, 1), jnp.float32)

        @pl.when(jnp.logical_not(first))
        def _():
            arrived(carried.at[m], carry_recv.at[m])

        for q in range(SPLIT):
            for k in range(1, dp):
                other = lax.rem(z + k, dp)
                arrived(landed.at[m, other, :, columns(q)], part_recv.at[m, q, other])
            branch = own[z, :, columns(q)]
            for k in range(1, dp):
                branch = branch + landed[m, lax.rem(z + k, dp), :, columns(q)].astype(jnp.float32)
            value = (carried[m, :, columns(q)].astype(jnp.float32) + branch).astype(jnp.bfloat16)
            out_ref[token_rows(m), columns(q)] = value
            value = value.astype(jnp.float32)
            residue = value - target_ref[token_rows(m), columns(q)].astype(jnp.float32)
            delta[m, z, :, columns(q)] = (error_scale / (micro * dp * tok) ** 0.5 * residue).astype(jnp.bfloat16)
            total = total + jnp.sum(value * value, axis=1, keepdims=True)
            squares = squares + jnp.sum(residue * residue, axis=1, keepdims=True)
        residue_ref[token_rows(m), :] = jnp.broadcast_to(squares, (tok, 128))

        @pl.when(inner)
        def _():
            stat_start(1, m, total)
            carry_copy(m).start()
            spread(m, out_ref, gain_next_ref, False)

    def carry_copy(m):
        return remote(
            out_ref.at[token_rows(m), :], carried.at[m], carry_sem.at[m], carry_recv.at[m], section + 1, z, t
        )

    for m in range(micro):
        receive_rows(m)
        rows_store(m).start()
        multiply(m)
        finish(m)
        for hop in range(min(dp, m + 1)):
            gather_step(m - hop, hop)
    for late in range(micro, micro + dp - 1):
        for hop in range(dp):
            if 0 <= late - hop < micro:
                gather_step(late - hop, hop)
    delta_store = pltpu.make_async_copy(delta, delta_hbm, store_sem.at[micro])
    delta_store.start()

    for m in range(micro):
        for q in range(SPLIT):
            for k in range(1, dp):
                part_copy(m, q, k).wait_send()
        for o in range(dp):

            @pl.when(t == o % nt)
            def _():
                for k in range(1, nt):
                    relay(m, o, k).wait_send()

            for way in (0, 1):
                onward = ((z + 1 < dp) & (o <= z)) if way else ((z >= 1) & (o >= z))

                @pl.when(onward)
                def _():
                    hand_on(m, o, way).wait_send()

        @pl.when(first)
        def _():
            for k in range(1, nt):
                left(stat.at[0, m, t], stat_send.at[0, m, k])
            for c in range(pieces):

                @pl.when(jnp.logical_not(at_home(c)))
                def _():
                    norm_copy(m, c, True).wait_send()

        @pl.when(inner)
        def _():
            for k in range(1, nt):
                left(stat.at[1, m, t], stat_send.at[1, m, k])
            carry_copy(m).wait_send()
            for c in range(pieces):
                norm_copy(m, c, False).wait_send()

        rows_store(m).wait()
    delta_store.wait()


def run_chain(activations, targets, weight, gain_row, gain_next, dp, nt):
    tok_dev, cols = activations.shape
    depth = weight.shape[0]
    tok = tok_dev // MICRO
    pieces = cols // depth
    bf16, f32 = jnp.bfloat16, jnp.float32
    vmem = pl.BlockSpec(memory_space=pltpu.VMEM)
    hbm = pl.BlockSpec(memory_space=pl.ANY)
    dma = pltpu.SemaphoreType.DMA
    out, residue, rows_all, delta_all = pl.pallas_call(
        chain_kernel,
        out_shape=(
            jax.ShapeDtypeStruct((tok_dev, cols), bf16),
            jax.ShapeDtypeStruct((tok_dev, 128), f32),
            jax.ShapeDtypeStruct((MICRO, dp, tok, depth), bf16),
            jax.ShapeDtypeStruct((MICRO, dp, tok, cols), bf16),
        ),
        in_specs=[vmem, vmem, hbm, vmem, vmem],
        out_specs=(vmem, vmem, hbm, hbm),
        scratch_shapes=[
            pltpu.VMEM((depth, cols), bf16),
            pltpu.VMEM((MICRO, dp, tok, depth), bf16),
            pltpu.VMEM((MICRO, dp, tok, cols), bf16),
            pltpu.VMEM((dp, tok, cols), f32),
            pltpu.VMEM((MICRO, dp, tok, cols), bf16),
            pltpu.VMEM((MICRO, tok, cols), bf16),
            pltpu.VMEM((MICRO, pieces, tok, depth), bf16),
            pltpu.VMEM((MICRO, pieces, tok, depth), bf16),
            pltpu.VMEM((2, MICRO, nt, tok, 128), f32),
            pltpu.VMEM((MICRO, dp, tok, cols), bf16),
            dma((SPLIT,)),
            dma((MICRO, dp)),
            dma((MICRO, dp, nt)),
            dma((MICRO, SPLIT, dp)),
            dma((MICRO, SPLIT, dp)),
            dma((MICRO,)),
            dma((MICRO,)),
            dma((MICRO, pieces)),
            dma((MICRO, pieces)),
            dma((2, MICRO, nt)),
            dma((2, MICRO, nt)),
            dma((MICRO, dp, 2)),
            dma((MICRO, dp)),
            dma((MICRO + 1,)),
        ],
        compiler_params=pltpu.CompilerParams(has_side_effects=True, vmem_limit_bytes=VMEM_ALL),
        cost_estimate=pl.CostEstimate(
            flops=2 * tok_dev * dp * depth * cols, transcendentals=0, bytes_accessed=2 * depth * cols
        ),
    )(activations, targets, weight, gain_row, gain_next)
    return out, residue[:, 0], rows_all.reshape(-1, depth), delta_all.reshape(-1, cols)


def passed_along(value, axis, steps):
    count = lax.axis_size(axis)
    leading, last = (max(0, -steps), min(count, count - steps))
    return lax.ppermute(value, axis, [(source, source + steps) for source in range(leading, last)])


def normalize(features, gain_row):
    inputs = features.astype(jnp.float32)
    mean_sq = jnp.mean(inputs * inputs, axis=1, keepdims=True)
    return (inputs * lax.rsqrt(mean_sq + norm_eps) * gain_row[None, :]).astype(jnp.bfloat16)


def ticked_chain(activations, targets, weight, gain_row):
    section_index = lax.axis_index("section")
    section_count = lax.axis_size("section")
    dp_count = lax.axis_size("dp")
    tok_dev, width_local = activations.shape
    token_total = tok_dev * dp_count
    tok_micro = tok_dev // MICRO
    received = jnp.zeros((tok_micro, width_local), jnp.bfloat16)
    row_ticks = []
    output_ticks = []
    tick_count = MICRO + section_count - 1
    for tick_index in range(tick_count):
        fed = min(tick_index, MICRO - 1) * tok_micro
        block_input = jnp.where(section_index == 0, activations[fed : fed + tok_micro], received)
        whole_rows = lax.all_gather(block_input, "tensor", axis=1, tiled=True)
        normed = normalize(whole_rows, gain_row)
        swapped = lax.all_to_all(normed, "dp", split_axis=1, concat_axis=0, tiled=True)
        partial_value = jnp.dot(swapped, weight, preferred_element_type=jnp.float32)
        branch = lax.psum_scatter(partial_value, "dp", scatter_dimension=0, tiled=True)
        block_result = (block_input.astype(jnp.float32) + branch).astype(jnp.bfloat16)
        row_ticks.append(swapped)
        output_ticks.append(block_result)
        if tick_index + 1 < tick_count:
            received = passed_along(block_result, "section", 1)
    stored_rows = lax.dynamic_slice_in_dim(jnp.stack(row_ticks), section_index, MICRO, axis=0)
    stored_rows = stored_rows.reshape(MICRO, dp_count, tok_micro, -1).transpose(1, 0, 2, 3)
    outputs_buf = lax.dynamic_slice_in_dim(
        jnp.concatenate(output_ticks), section_index * tok_micro, tok_dev, axis=0
    )
    residue = outputs_buf.astype(jnp.float32) - targets.astype(jnp.float32)
    delta = (error_scale / token_total**0.5 * residue).astype(jnp.bfloat16)
    delta_all = lax.all_gather(delta, "dp", axis=0, tiled=True)
    rows_all = stored_rows.reshape(dp_count * tok_dev, -1)
    return outputs_buf, jnp.sum(residue * residue, axis=1), rows_all, delta_all


def per_device(activations, targets, packed_floors, rounding, scales, norm_gains):
    dp_count = lax.axis_size("dp")
    core_count = lax.axis_size("tensor")
    tok_dev, width_local = activations.shape
    width_full = norm_gains.shape[1]
    token_total = tok_dev * dp_count
    weight = make_weight(packed_floors[0], rounding[0], scales)
    if width_local % rounding.shape[1] == 0 and dp_count % core_count == 0:
        here = lax.axis_index("tensor") * width_local
        gain_row = lax.dynamic_slice_in_dim(norm_gains, here, width_local, axis=1)
        gain_next = passed_along(gain_row, "section", -1)
        outputs_buf, residues, rows_all, delta_all = run_chain(
            activations, targets[0], weight, gain_row, gain_next, dp_count, core_count
        )
    else:
        outputs_buf, residues, rows_all, delta_all = ticked_chain(
            activations, targets[0], weight, norm_gains[0]
        )
    grad, sums = make_grad(rows_all, delta_all, rounding[0], scales)
    recon_sum, penalty_sum, square_sum = lax.psum(
        (jnp.sum(residues), jnp.sum(sums[1]), jnp.sum(sums[0])), ("dp", "tensor")
    )
    mean_grad = square_sum / (width_full * width_full) + grad_eps
    rounding_next = rounding[0] - step_rate * grad.astype(jnp.float32) * lax.rsqrt(mean_grad)
    loss_value = recon_sum / (token_total * width_full) + reg_weight * penalty_sum / (
        width_full * width_full
    )
    return (rounding_next[None], outputs_buf[None], loss_value.reshape(1))


def solution(mesh):
    placed = (
        P("dp", "tensor"),
        P("section", "dp", "tensor"),
        P("section", "dp", "tensor"),
        P("section", "dp", "tensor"),
        P("section", "tensor"),
        P("section", None),
    )
    return jax.shard_map(
        per_device,
        mesh=mesh,
        in_specs=placed,
        out_specs=(P("section", "dp", "tensor"), P("section", "dp", "tensor"), P("section")),
        check_vma=False,
    )
```

time: 887 us -> 468 us (0.53)
  Pallas kernels: 0 us -> 414 us
  waiting for transfers between devices: 406 us -> 0.01 us
  blocking collectives: 151 us -> 14.2 us
  matrix products: 106 us -> 0 us
  other arithmetic: 122 us -> 30.2 us
  local copies, waits for them, and re-layouts: 64.7 us -> 2.33 us
  between operations: 17.9 us -> 3.73 us
  starting transfers between devices: 12.7 us -> 2.15 us
    pallas_call x0 -> x3, Pallas kernels: none -> 414 us  [the longest x1 332 us: run_chain(): pl.pallas_call(chain_kernel, out_shape=(jax.ShapeDtypeStruct((tok_dev, co...]
    reduce_scatter x7 -> x0, waiting for transfers between devices: 303 us -> none  [per_device(): lax.psum_scatter(partial_value, 'dp', scatter_dimension=0, tiled=True)]
    all_to_all x6 -> x0, blocking collectives: 111 us -> none  [per_device(): lax.all_to_all(normed, 'dp', split_axis=1, concat_axis=0, tiled=True)]
    dot_general x8 -> x0, matrix products: 106 us -> none  [the longest x7 66.1 us: per_device(): jnp.dot(swapped, soft_weight, preferred_element_type=jnp.float32)]
    all_gather x1 -> x0, waiting for transfers between devices: 59 us -> none  [per_device(): delta_all = lax.all_gather(delta, 'dp', axis=0, tiled=True)]
    ppermute x6 -> x1, waiting for transfers between devices: 44.3 us -> 0.01 us  [passed_along(): lax.ppermute(value, axis, [(source, source + steps) for source in range(l...]
    min x1 -> x0, local copies, waits for them, and re-layouts: 37.4 us -> none  [soft_round(): soft_part = jnp.clip(linear, 0.0, 1.0)]
    min x1 -> x0, other arithmetic: 25.2 us -> none  [soft_round(): soft_part = jnp.clip(linear, 0.0, 1.0)]
  transfers between devices with their start and end apart: 15 -> 1, of which waited for: 14 -> 0; matrix products, arithmetic and copies ran while one was open for 15% -> 0% of each run, Pallas kernels for 0% -> 7%
where the time goes in v1:
time: 468 us; the launch traced here: 467 us
  Pallas kernels  414 us (88%)
  other arithmetic  30.2 us (6%)
  blocking collectives  14.2 us (3%)
    pallas_call x1, Pallas kernels, run_chain(): pl.pallas_call(chain_kernel, out_shape=(jax.ShapeDtypeStruct((tok_dev, co...  332 us
    pallas_call x1, Pallas kernels, make_grad(): pl.pallas_call(grad_kernel, out_shape=(jax.ShapeDtypeStruct((rows, cols),...  49.1 us
    pallas_call x1, Pallas kernels, make_weight(): pl.pallas_call(weight_kernel, out_shape=jax.ShapeDtypeStruct((rows, cols)...  32.6 us
    broadcast_in_dim x1, other arithmetic, per_device(): return (rounding_next[None], outputs_buf[None], loss_value.reshape(1))  27.4 us
    psum x1, blocking collectives, per_device(): lax.psum((jnp.sum(residues), jnp.sum(sums[1]), jnp.sum(sums[0])), ('dp',...  14.2 us
  transfers between devices with their start and end apart: 1, of which 0 were waited for; matrix products, arithmetic and copies ran while one was open for 0% of the time, Pallas kernels for 7%

profile of v1, /device:TPU:7, one launch (start us, length us, event | category | flops | bytes accessed | tf_op | source)
XLA Modules:
  0.0 466.7 jit_solution(3154317552973178657)
XLA Ops:
  0.6 0.0 copy-start
  0.7 0.7 copy-done
  1.4 0.0 copy-start.3
  1.4 2.1 collective-permute-start
  3.6 32.6 %shard_map.85.weight_hbm = bf16[2048,4096]{1,0:T(8,128)(2,1)} custom-call(s32[512,4096]{1,0:T(8,128)} %bitcast.12, f32[2048,4096]{1,0:T(8,128)} %bitcast.10, f32[1,4096]{1,0:T(1,128)} %scale_ref.3), custom_call_target="tpu_custom_call" | custom-call | flops 167772160 | bytes 58720256 | tf_op jit(solution)/shard_map/pallas_call | solution.py:53
  36.2 0.0 collective-permute-done.gain_next_ref
  36.2 0.0 copy-start.4
  36.2 0.0 copy-done.3
  36.2 0.6 copy-done.4
  36.8 332.4 %shard_map.86 = (bf16[128,4096]{1,0:T(8,128)(2,1)}, f32[128,128]{1,0:T(8,128)}, bf16[4,4,32,2048]{3,2,1,0:T(8,128)(2,1)}, bf16[4,4,32,4096]{3,2,1,0:T(8,128)(2,1)}) custom-call(bf16[128,4096]{1,0:T(8,128)(2,1)} %act_ref.1, bf16[128,4096]{1,0:T(8,128)(2,1)} %bitcast.16, bf16[2048,4096]{1,0:T(8,128)(2,1)} %shard_map.85.weight_hbm, f32[1,4096]{1,0:T(1,128)} %copy-done.3, ...), custom_call_target="tpu_custom_call" | custom-call | flops 8589934592 | bytes 16777216 | tf_op jit(solution)/shard_map/pallas_call | solution.py:413
  369.2 1.5 slice_reduce_fusion
  370.7 49.1 %shard_map.87 = (bf16[2048,4096]{1,0:T(8,128)(2,1)}, f32[2,8,128]{2,1,0:T(8,128)}) custom-call(bf16[512,2048]{1,0:T(8,128)(2,1)} %bitcast.14, bf16[512,4096]{1,0:T(8,128)(2,1)} %bitcast.13, f32[2048,4096]{1,0:T(8,128)} %bitcast.11, f32[1,4096]{1,0:T(1,128)} %scale_ref.3), custom_call_target="tpu_custom_call" | custom-call | flops 8589934592 | bytes 50331648 | tf_op jit(solution)/shard_map/pallas_call | solution.py:112
  419.7 1.3 slice_reduce_fusion.1
  421.0 14.2 %all-reduce = (f32[]{:T(128)}, f32[]{:T(128)}, f32[]{:T(128)}) all-reduce(f32[]{:T(128)} %get-tuple-element.16, f32[]{:T(128)} %slice_reduce_fusion, f32[]{:T(128)} %get-tuple-element.15), channel_id=1, replica_groups=mesh['section'=4,'dp'=4,'tensor'=2] {'dp','tensor'}, use_global_device_ids=true, to_apply=%region_1.0 | all-reduce | flops 3 | bytes 24 | tf_op jit(solution)/shard_map/psum | solution.py:524
  437.2 0.0 copy-start.1
  437.2 0.0 copy-start.2
  437.2 27.4 %subtract_bitcast_fusion = f32[1,2048,4096]{2,1,0:T(8,128)} fusion(bf16[2048,4096]{1,0:T(8,128)(2,1)} %get-tuple-element.11, f32[]{:T(128)S(6)} %mul.14, f32[1,2048,4096]{2,1,0:T(8,128)} %param.9), kind=kLoop, calls=%fused_computation | loop fusion | flops 25165824 | bytes 83886080 | tf_op jit(solution)/shard_map/broadcast_in_dim | solution.py:532
  464.6 0.0 copy-done.2
  464.6 1.0 copy.10
  465.6 0.0 copy-done.1
  (1 shorter events, 0.0 us)
Async XLA Ops:
  0.6 0.8 copy-start
  1.4 34.8 %copy-start.3 = (f32[1,4096]{1,0:T(1,128)}, f32[1,4096]{1,0:T(1,128)S(1)}, u32[]{:S(2)}) copy-start(f32[1,4096]{1,0:T(1,128)S(1)} %constant_dynamic-slice_fusion.gain_ref) | copy-start | bytes 49156
  1.4 34.8 %collective-permute-start = (f32[1,4096]{1,0:T(1,128)S(1)}, f32[1,4096]{1,0:T(1,128)S(1)}, u32[]{:S(2)}, u32[]{:S(2)}) collective-permute-start(f32[1,4096]{1,0:T(1,128)S(1)} %constant_dynamic-slice_fusion.gain_ref), channel_id=1, source_target_pairs={{8,0},{16,8},{24,16},{9,1},{17,9},{25,17},{10,2},{18,10},{26,18},{... | collective-permute-start | bytes 49160 | tf_op jit(solution)/shard_map/ppermute | solution.py:460
  36.2 0.6 copy-start.4
  437.2 28.4 %copy-start.1 = (f32[1,8192]{1,0:T(1,128)S(1)}, f32[1,8192]{1,0:T(1,128)}, u32[]{:S(2)}) copy-start(f32[1,8192]{1,0:T(1,128)} %param.11) | copy-start | bytes 98308
  437.2 27.4 %copy-start.2 = (bf16[128,4096]{1,0:T(8,128)(2,1)S(1)}, bf16[128,4096]{1,0:T(8,128)(2,1)}, u32[]{:S(2)}) copy-start(bf16[128,4096]{1,0:T(8,128)(2,1)} %get-tuple-element.13) | copy-start | bytes 3145732

commit v2 on v1

--- a/solution.py
+++ b/solution.py
@@ -6,7 +6,8 @@
 from jax.experimental.pallas import tpu as pltpu
 from jax.sharding import PartitionSpec as P
 
-MICRO = 4
+MICRO = 8
+TICKS = 4
 SPLIT = 4
 
 
@@ -89,10 +90,9 @@
         def strip(rb, sums):
             row = pl.ds(pl.multiple_of(rb * strip_r, strip_r), strip_r)
             full = 1.2 * jnp.tanh(0.5 * rounding_ref[row, col])
-            inside = jnp.abs(full) < 1.0
             polarity = jnp.clip(full, -1.0, 1.0)
             square = polarity * polarity
-            slope = jnp.where(inside, 0.3 - (0.3 / 1.44) * square, 0.0)
+            slope = jnp.where(square < 1.0, 0.3 - (0.3 / 1.44) * square, 0.0)
             grad = slope * (scale * product[row, col] - (8.0 * reg_weight) * (square * polarity))
             grad_ref[row, col] = grad.astype(grad_ref.dtype)
             fold = lambda v: v.reshape(strip_r // 8, 8, strip_c).sum(axis=0)
@@ -137,8 +137,8 @@
 def chain_kernel(
     act_ref, target_ref, weight_hbm, gain_ref, gain_next_ref,
     out_ref, residue_ref, rows_hbm, delta_hbm,
-    weight, rows, part, own, landed, carried, normed, normed0, stat, delta,
-    w_sem, row_sem, relay_sem, part_send, part_recv, carry_sem, carry_recv,
+    weight, rows, part, own, landed, joined, carried, normed, normed0, stat, delta,
+    w_sem, row_sem, relay_sem, mate_send, join_send, join_recv, land_send, land_recv, carry_sem, carry_recv,
     norm_send, norm0_send, stat_send, stat_recv, delta_send, delta_recv, store_sem,
 ):
     section, z, t = (lax.axis_index(name) for name in ("section", "dp", "tensor"))
@@ -266,11 +266,28 @@
     def rows_store(m):
         return pltpu.make_async_copy(rows.at[m], rows_hbm.at[m], store_sem.at[m])
 
-    def part_copy(m, q, k):
-        to = lax.rem(z + k, dp)
+    side = dp // 2
+    place = lax.rem(z, side)
+    across = (1 - z // side) * side
+    is_inner = place == (side - 1) * (1 - z // side)
+    inner_here = jnp.where(z < side, side - 1, side)
+
+    def mate_copy(m, k):
+        mate = z - place + lax.rem(place + k, side)
         return remote(
-            part.at[m, to, :, columns(q)], landed.at[m, z, :, columns(q)],
-            part_send.at[m, q, k], part_recv.at[m, q, z], section, to, t,
+            part.at[m, mate], landed.at[m, place], mate_send.at[m, k], land_recv.at[m, 0, place], section, mate, t
+        )
+
+    def join_copy(m, q, o):
+        return remote(
+            part.at[m, across + o, :, columns(q)], joined.at[m, place, o, :, columns(q)],
+            join_send.at[m, q, o], join_recv.at[m, q, place, o], section, inner_here, t,
+        )
+
+    def land_copy(m, q, o):
+        return remote(
+            part.at[m, across + o, :, columns(q)], landed.at[m, o, :, columns(q)],
+            land_send.at[m, q, o], land_recv.at[m, q, o], section, across + o, t,
         )
 
     def multiply(m):
@@ -285,11 +302,29 @@
                 value = jnp.dot(
                     rows[m].reshape(dp * tok, depth), weight[:, cut], preferred_element_type=jnp.float32
                 )
-                own[:, :, cut] = value.reshape(dp, tok, step)
+                own[m % 2, :, :, cut] = value.reshape(dp, tok, step)
                 part[m, :, :, cut] = value.reshape(dp, tok, step).astype(jnp.bfloat16)
 
-            for k in range(1, dp):
-                part_copy(m, q, k).start()
+            @pl.when(jnp.logical_not(is_inner))
+            def _():
+                for o in range(side):
+                    join_copy(m, q, o).start()
+
+        for k in range(1, side):
+            mate_copy(m, k).start()
+
+    def combine(m):
+        @pl.when(is_inner)
+        def _():
+            for q in range(SPLIT):
+                for o in range(side):
+                    total = own[m % 2, across + o, :, columns(q)]
+                    for k in range(1, side):
+                        mate = lax.rem(place + k, side)
+                        arrived(joined.at[m, mate, o, :, columns(q)], join_recv.at[m, q, mate, o])
+                        total = total + joined[m, mate, o, :, columns(q)].astype(jnp.float32)
+                    part[m, across + o, :, columns(q)] = total.astype(jnp.bfloat16)
+                    land_copy(m, q, o).start()
 
     def hand_on(m, origin, way):
         return remote(
@@ -321,12 +356,14 @@
             arrived(carried.at[m], carry_recv.at[m])
 
         for q in range(SPLIT):
-            for k in range(1, dp):
-                other = lax.rem(z + k, dp)
-                arrived(landed.at[m, other, :, columns(q)], part_recv.at[m, q, other])
-            branch = own[z, :, columns(q)]
-            for k in range(1, dp):
-                branch = branch + landed[m, lax.rem(z + k, dp), :, columns(q)].astype(jnp.float32)
+            arrived(landed.at[m, place, :, columns(q)], land_recv.at[m, q, place])
+            if q == 0:
+                for k in range(1, side):
+                    mate = lax.rem(place + k, side)
+                    arrived(landed.at[m, mate], land_recv.at[m, 0, mate])
+            branch = own[m % 2, z, :, columns(q)]
+            for k in range(side):
+                branch = branch + landed[m, lax.rem(place + k, side), :, columns(q)].astype(jnp.float32)
             value = (carried[m, :, columns(q)].astype(jnp.float32) + branch).astype(jnp.bfloat16)
             out_ref[token_rows(m), columns(q)] = value
             value = value.astype(jnp.float32)
@@ -347,13 +384,19 @@
             out_ref.at[token_rows(m), :], carried.at[m], carry_sem.at[m], carry_recv.at[m], section + 1, z, t
         )
 
+    def complete(m):
+        finish(m)
+        for hop in range(min(dp, m + 1)):
+            gather_step(m - hop, hop)
+
     for m in range(micro):
         receive_rows(m)
         rows_store(m).start()
         multiply(m)
-        finish(m)
-        for hop in range(min(dp, m + 1)):
-            gather_step(m - hop, hop)
+        if m:
+            complete(m - 1)
+        combine(m)
+    complete(micro - 1)
     for late in range(micro, micro + dp - 1):
         for hop in range(dp):
             if 0 <= late - hop < micro:
@@ -362,9 +405,19 @@
     delta_store.start()
 
     for m in range(micro):
+        for k in range(1, side):
+            mate_copy(m, k).wait_send()
         for q in range(SPLIT):
-            for k in range(1, dp):
-                part_copy(m, q, k).wait_send()
+            for o in range(side):
+
+                @pl.when(is_inner)
+                def _():
+                    land_copy(m, q, o).wait_send()
+
+                @pl.when(jnp.logical_not(is_inner))
+                def _():
+                    join_copy(m, q, o).wait_send()
+
         for o in range(dp):
 
             @pl.when(t == o % nt)
@@ -406,6 +459,7 @@
     depth = weight.shape[0]
     tok = tok_dev // MICRO
     pieces = cols // depth
+    side = dp // 2
     bf16, f32 = jnp.bfloat16, jnp.float32
     vmem = pl.BlockSpec(memory_space=pltpu.VMEM)
     hbm = pl.BlockSpec(memory_space=pl.ANY)
@@ -424,8 +478,9 @@
             pltpu.VMEM((depth, cols), bf16),
             pltpu.VMEM((MICRO, dp, tok, depth), bf16),
             pltpu.VMEM((MICRO, dp, tok, cols), bf16),
-            pltpu.VMEM((dp, tok, cols), f32),
-            pltpu.VMEM((MICRO, dp, tok, cols), bf16),
+            pltpu.VMEM((2, dp, tok, cols), f32),
+            pltpu.VMEM((MICRO, side, tok, cols), bf16),
+            pltpu.VMEM((MICRO, side, side, tok, cols), bf16),
             pltpu.VMEM((MICRO, tok, cols), bf16),
             pltpu.VMEM((MICRO, pieces, tok, depth), bf16),
             pltpu.VMEM((MICRO, pieces, tok, depth), bf16),
@@ -434,8 +489,11 @@
             dma((SPLIT,)),
             dma((MICRO, dp)),
             dma((MICRO, dp, nt)),
-            dma((MICRO, SPLIT, dp)),
-            dma((MICRO, SPLIT, dp)),
+            dma((MICRO, side)),
+            dma((MICRO, SPLIT, side)),
+            dma((MICRO, SPLIT, side, side)),
+            dma((MICRO, SPLIT, side)),
+            dma((MICRO, SPLIT, side)),
             dma((MICRO,)),
             dma((MICRO,)),
             dma((MICRO, pieces)),
@@ -451,7 +509,54 @@
             flops=2 * tok_dev * dp * depth * cols, transcendentals=0, bytes_accessed=2 * depth * cols
         ),
     )(activations, targets, weight, gain_row, gain_next)
-    return out, residue[:, 0], rows_all.reshape(-1, depth), delta_all.reshape(-1, cols)
+    return out, residue, rows_all.reshape(-1, depth), delta_all.reshape(-1, cols)
+
+
+def sums_kernel(mine_ref, total_ref, held, send_sem, recv_sem):
+    z, t = lax.axis_index("dp"), lax.axis_index("tensor")
+    dp, nt = lax.axis_size("dp"), lax.axis_size("tensor")
+    place = z * nt + t
+    count = dp * nt
+
+    def copy(k):
+        peer = lax.rem(place + k, count)
+        return pltpu.make_async_remote_copy(
+            src_ref=mine_ref, dst_ref=held.at[place], send_sem=send_sem.at[k], recv_sem=recv_sem.at[place],
+            device_id={"dp": peer // nt, "tensor": lax.rem(peer, nt)}, device_id_type=pl.DeviceIdType.MESH,
+        )
+
+    for k in range(1, count):
+        copy(k).start()
+    held[place] = mine_ref[...]
+    for k in range(1, count):
+        peer = lax.rem(place + k, count)
+        pltpu.make_async_remote_copy(
+            src_ref=mine_ref, dst_ref=held.at[peer], send_sem=send_sem.at[k], recv_sem=recv_sem.at[peer],
+            device_id={"dp": z, "tensor": t}, device_id_type=pl.DeviceIdType.MESH,
+        ).wait_recv()
+    total = held[0]
+    for k in range(1, count):
+        total = total + held[k]
+    total = jnp.sum(total, axis=1, keepdims=True)
+    total_ref[...] = jnp.broadcast_to(jnp.sum(total, axis=2, keepdims=True), total_ref.shape)
+    for k in range(1, count):
+        copy(k).wait_send()
+
+
+def add_sums(mine, count):
+    vmem = pl.BlockSpec(memory_space=pltpu.VMEM)
+    return pl.pallas_call(
+        sums_kernel,
+        out_shape=jax.ShapeDtypeStruct(mine.shape, mine.dtype),
+        in_specs=[vmem],
+        out_specs=vmem,
+        scratch_shapes=[
+            pltpu.VMEM((count,) + mine.shape, mine.dtype),
+            pltpu.SemaphoreType.DMA((count,)),
+            pltpu.SemaphoreType.DMA((count,)),
+        ],
+        compiler_params=pltpu.CompilerParams(has_side_effects=True),
+    )(mine)[:, 0, 0]
 
 
 def passed_along(value, axis, steps):
@@ -472,13 +577,13 @@
     dp_count = lax.axis_size("dp")
     tok_dev, width_local = activations.shape
     token_total = tok_dev * dp_count
-    tok_micro = tok_dev // MICRO
+    tok_micro = tok_dev // TICKS
     received = jnp.zeros((tok_micro, width_local), jnp.bfloat16)
     row_ticks = []
     output_ticks = []
-    tick_count = MICRO + section_count - 1
+    tick_count = TICKS + section_count - 1
     for tick_index in range(tick_count):
-        fed = min(tick_index, MICRO - 1) * tok_micro
+        fed = min(tick_index, TICKS - 1) * tok_micro
         block_input = jnp.where(section_index == 0, activations[fed : fed + tok_micro], received)
         whole_rows = lax.all_gather(block_input, "tensor", axis=1, tiled=True)
         normed = normalize(whole_rows, gain_row)
@@ -490,8 +595,8 @@
         output_ticks.append(block_result)
         if tick_index + 1 < tick_count:
             received = passed_along(block_result, "section", 1)
-    stored_rows = lax.dynamic_slice_in_dim(jnp.stack(row_ticks), section_index, MICRO, axis=0)
-    stored_rows = stored_rows.reshape(MICRO, dp_count, tok_micro, -1).transpose(1, 0, 2, 3)
+    stored_rows = lax.dynamic_slice_in_dim(jnp.stack(row_ticks), section_index, TICKS, axis=0)
+    stored_rows = stored_rows.reshape(TICKS, dp_count, tok_micro, -1).transpose(1, 0, 2, 3)
     outputs_buf = lax.dynamic_slice_in_dim(
         jnp.concatenate(output_ticks), section_index * tok_micro, tok_dev, axis=0
     )
@@ -509,7 +614,8 @@
     width_full = norm_gains.shape[1]
     token_total = tok_dev * dp_count
     weight = make_weight(packed_floors[0], rounding[0], scales)
-    if width_local % rounding.shape[1] == 0 and dp_count % core_count == 0:
+    chained = width_local % rounding.shape[1] == 0 and dp_count % core_count == 0 and dp_count % 2 == 0
+    if chained:
         here = lax.axis_index("tensor") * width_local
         gain_row = lax.dynamic_slice_in_dim(norm_gains, here, width_local, axis=1)
         gain_next = passed_along(gain_row, "section", -1)
@@ -521,9 +627,16 @@
             activations, targets[0], weight, norm_gains[0]
         )
     grad, sums = make_grad(rows_all, delta_all, rounding[0], scales)
-    recon_sum, penalty_sum, square_sum = lax.psum(
-        (jnp.sum(residues), jnp.sum(sums[1]), jnp.sum(sums[0])), ("dp", "tensor")
-    )
+    if chained:
+        recon = jnp.where(lax.broadcasted_iota(jnp.int32, residues.shape, 1) == 0, residues, 0.0)
+        recon = recon.reshape(-1, 8, 128).sum(axis=0)
+        square_sum, penalty_sum, recon_sum = add_sums(
+            jnp.concatenate([sums, recon[None]]), dp_count * core_count
+        )
+    else:
+        recon_sum, penalty_sum, square_sum = lax.psum(
+            (jnp.sum(residues), jnp.sum(sums[1]), jnp.sum(sums[0])), ("dp", "tensor")
+        )
     mean_grad = square_sum / (width_full * width_full) + grad_eps
     rounding_next = rounding[0] - step_rate * grad.astype(jnp.float32) * lax.rsqrt(mean_grad)
     loss_value = recon_sum / (token_total * width_full) + reg_weight * penalty_sum / (

time: 468 us -> 410 us (0.88)
  Pallas kernels: 414 us -> 369 us
  blocking collectives: 14.2 us -> 0 us
    pallas_call x1, Pallas kernels: 332 us -> 277 us  [run_chain(): pl.pallas_call(chain_kernel, out_shape=(jax.ShapeDtypeStruct((tok_dev, co...]
    psum x1 -> x0, blocking collectives: 14.2 us -> none  [per_device(): lax.psum((jnp.sum(residues), jnp.sum(sums[1]), jnp.sum(sums[0])), ('dp',...]
    pallas_call x0 -> x1, Pallas kernels: none -> 10.4 us  [add_sums(): pl.pallas_call(sums_kernel, out_shape=jax.ShapeDtypeStruct(mine.shape, mi...]
  transfers between devices with their start and end apart: 1 -> 1, of which waited for: 0 -> 0; matrix products, arithmetic and copies ran while one was open for 0% -> 0% of each run, Pallas kernels for 7% -> 8%
where the time goes in v2:
time: 410 us; the launch traced here: 408 us
  Pallas kernels  369 us (90%)
  other arithmetic  29.6 us (7%)
    pallas_call x1, Pallas kernels, run_chain(): pl.pallas_call(chain_kernel, out_shape=(jax.ShapeDtypeStruct((tok_dev, co...  277 us
    pallas_call x1, Pallas kernels, make_grad(): pl.pallas_call(grad_kernel, out_shape=(jax.ShapeDtypeStruct((rows, cols),...  48.7 us
    pallas_call x1, Pallas kernels, make_weight(): pl.pallas_call(weight_kernel, out_shape=jax.ShapeDtypeStruct((rows, cols)...  32.6 us
    broadcast_in_dim x1, other arithmetic, per_device(): return (rounding_next[None], outputs_buf[None], loss_value.reshape(1))  27.4 us
    pallas_call x1, Pallas kernels, add_sums(): pl.pallas_call(sums_kernel, out_shape=jax.ShapeDtypeStruct(mine.shape, mi...  10.4 us
  transfers between devices with their start and end apart: 1, of which 0 were waited for; matrix products, arithmetic and copies ran while one was open for 0% of the time, Pallas kernels for 8%

profile of v2, /device:TPU:7, one launch (start us, length us, event | category | flops | bytes accessed | tf_op | source)
XLA Modules:
  0.0 407.6 jit_solution(16837935380715958230)
XLA Ops:
  0.6 0.0 copy-start
  0.7 0.7 copy-done
  1.4 0.0 copy-start.3
  1.4 2.1 collective-permute-start
  3.6 32.6 %shard_map.85.weight_hbm = bf16[2048,4096]{1,0:T(8,128)(2,1)} custom-call(s32[512,4096]{1,0:T(8,128)} %bitcast.16, f32[2048,4096]{1,0:T(8,128)} %bitcast.14, f32[1,4096]{1,0:T(1,128)} %scale_ref.3), custom_call_target="tpu_custom_call" | custom-call | flops 167772160 | bytes 58720256 | tf_op jit(solution)/shard_map/pallas_call | solution.py:54
  36.2 0.0 collective-permute-done.gain_next_ref
  36.2 0.0 copy-start.4
  36.2 0.0 copy-done.3
  36.2 0.6 copy-done.4
  36.8 276.8 %shard_map.86 = (bf16[128,4096]{1,0:T(8,128)(2,1)}, f32[128,128]{1,0:T(8,128)}, bf16[8,4,16,2048]{3,2,1,0:T(8,128)(2,1)}, bf16[8,4,16,4096]{3,2,1,0:T(8,128)(2,1)}) custom-call(bf16[128,4096]{1,0:T(8,128)(2,1)} %act_ref.1, bf16[128,4096]{1,0:T(8,128)(2,1)} %bitcast.21, bf16[2048,4096]{1,0:T(8,128)(2,1)} %shard_map.85.weight_hbm, f32[1,4096]{1,0:T(1,128)} %copy-done.3, ...), custom_call_target="tpu_custom_call" | custom-call | flops 8589934592 | bytes 16777216 | tf_op jit(solution)/shard_map/pallas_call | solution.py:467
  313.6 0.9 bitcast_reduce_fusion
  314.5 48.7 %shard_map.87 = (bf16[2048,4096]{1,0:T(8,128)(2,1)}, f32[2,8,128]{2,1,0:T(8,128)}) custom-call(bf16[512,2048]{1,0:T(8,128)(2,1)} %bitcast.18, bf16[512,4096]{1,0:T(8,128)(2,1)} %bitcast.17, f32[2048,4096]{1,0:T(8,128)} %bitcast.15, f32[1,4096]{1,0:T(1,128)} %scale_ref.3), custom_call_target="tpu_custom_call" | custom-call | flops 8589934592 | bytes 50331648 | tf_op jit(solution)/shard_map/pallas_call | solution.py:112
  363.2 1.3 pad_maximum_fusion.mine_ref
  364.5 10.4 %shard_map.88 = f32[3,8,128]{2,1,0:T(8,128)} custom-call(f32[3,8,128]{2,1,0:T(8,128)} %pad_maximum_fusion.mine_ref), custom_call_target="tpu_custom_call" | custom-call | tf_op jit(solution)/shard_map/pallas_call | solution.py:548
  374.9 1.2 fusion
  378.1 0.0 copy-start.1
  378.1 0.0 copy-start.2
  378.1 27.4 %subtract_bitcast_fusion = f32[1,2048,4096]{2,1,0:T(8,128)} fusion(bf16[2048,4096]{1,0:T(8,128)(2,1)} %get-tuple-element.11, f32[]{:T(128)} %bitcast.7, f32[1,2048,4096]{2,1,0:T(8,128)} %param.9), kind=kLoop, calls=%fused_computation | loop fusion | flops 25165824 | bytes 83886080 | tf_op jit(solution)/shard_map/broadcast_in_dim | solution.py:645
  405.5 0.0 copy-done.2
  405.5 1.0 copy.10
  406.5 0.0 copy-done.1
  (2 shorter events, 0.0 us)
Async XLA Ops:
  0.6 0.8 copy-start
  1.4 34.8 %copy-start.3 = (f32[1,4096]{1,0:T(1,128)}, f32[1,4096]{1,0:T(1,128)S(1)}, u32[]{:S(2)}) copy-start(f32[1,4096]{1,0:T(1,128)S(1)} %constant_dynamic-slice_fusion.gain_ref) | copy-start | bytes 49156
  1.4 34.8 %collective-permute-start = (f32[1,4096]{1,0:T(1,128)S(1)}, f32[1,4096]{1,0:T(1,128)S(1)}, u32[]{:S(2)}, u32[]{:S(2)}) collective-permute-start(f32[1,4096]{1,0:T(1,128)S(1)} %constant_dynamic-slice_fusion.gain_ref), channel_id=1, source_target_pairs={{8,0},{16,8},{24,16},{9,1},{17,9},{25,17},{10,2},{18,10},{26,18},{... | collective-permute-start | bytes 49160 | tf_op jit(solution)/shard_map/ppermute | solution.py:565
  36.2 0.6 copy-start.4
  378.1 28.4 %copy-start.1 = (f32[1,8192]{1,0:T(1,128)S(1)}, f32[1,8192]{1,0:T(1,128)}, u32[]{:S(2)}) copy-start(f32[1,8192]{1,0:T(1,128)} %param.11) | copy-start | bytes 98308
  378.1 27.4 %copy-start.2 = (bf16[128,4096]{1,0:T(8,128)(2,1)S(1)}, bf16[128,4096]{1,0:T(8,128)(2,1)}, u32[]{:S(2)}) copy-start(bf16[128,4096]{1,0:T(8,128)(2,1)} %get-tuple-element.14) | copy-start | bytes 3145732

commit v3 on v2

--- a/solution.py
+++ b/solution.py
@@ -9,6 +9,7 @@
 MICRO = 8
 TICKS = 4
 SPLIT = 4
+LAG = 2
 
 
 norm_eps = 1e-06
@@ -28,24 +29,32 @@
 
 def weight_kernel(packed_ref, rounding_ref, scale_ref, weight_ref):
     rows, cols = rounding_ref.shape
-    strip_c = tile_of(cols, 512)
+    strip_c = tile_of(cols, 1024)
     strip_r = 32
 
     @pl.loop(0, cols // strip_c)
     def _(cb):
         col = pl.ds(pl.multiple_of(cb * strip_c, strip_c), strip_c)
         scale = scale_ref[:, col]
-        shift = 3 * (lax.broadcasted_iota(jnp.int32, (strip_r, strip_c), 0) & 3)
+        place = lax.broadcasted_iota(jnp.int32, (8, strip_c), 0)
+        shift = 3 * (place & 3)
+        upper = place < 4
 
         @pl.loop(0, rows // strip_r)
         def _(rb):
+            values = []
+            for k in range(strip_r // 8):
+                row = pl.ds(pl.multiple_of(rb * strip_r, strip_r) + 8 * k, 8)
+                first = packed_ref[pl.ds(rb * (strip_r // 4) + 2 * k, 1), col]
+                second = packed_ref[pl.ds(rb * (strip_r // 4) + 2 * k + 1, 1), col]
+                words = jnp.where(
+                    upper, jnp.broadcast_to(first, upper.shape), jnp.broadcast_to(second, upper.shape)
+                )
+                codes = (jnp.right_shift(words, shift) & 7).astype(jnp.float32)
+                part = jnp.clip(0.6 * jnp.tanh(0.5 * rounding_ref[row, col]) - 3.5, -4.0, -3.0)
+                values.append(scale * (codes + part))
             row = pl.ds(pl.multiple_of(rb * strip_r, strip_r), strip_r)
-            word = pl.ds(pl.multiple_of(rb * (strip_r // 4), strip_r // 4), strip_r // 4)
-            words = jnp.repeat(packed_ref[word, col], 4, axis=0)
-            codes = (jnp.right_shift(words, shift) & 7).astype(jnp.float32)
-            half = jnp.tanh(0.5 * rounding_ref[row, col])
-            soft = jnp.clip(0.6 * half + 0.5, 0.0, 1.0)
-            weight_ref[row, col] = (scale * ((codes - 4.0) + soft)).astype(jnp.bfloat16)
+            weight_ref[row, col] = jnp.concatenate(values, axis=0).astype(jnp.bfloat16)
 
 
 def make_weight(packed, rounding, scale_row):
@@ -71,7 +80,7 @@
 def grad_kernel(rows_ref, delta_ref, rounding_ref, scale_ref, grad_ref, sums_ref, product):
     trow, tcol = rounding_ref.shape
     strip_c = tile_of(tcol, 512)
-    strip_r = 16
+    strip_r = 64
     first = (pl.program_id(0) == 0) & (pl.program_id(1) == 0)
 
     @pl.when(first)
@@ -85,18 +94,17 @@
     @pl.loop(0, tcol // strip_c)
     def _(cb):
         col = pl.ds(pl.multiple_of(cb * strip_c, strip_c), strip_c)
-        scale = scale_ref[:, col]
+        scale = (0.3 / 1.44 / 4.0) * scale_ref[:, col]
 
         def strip(rb, sums):
             row = pl.ds(pl.multiple_of(rb * strip_r, strip_r), strip_r)
-            full = 1.2 * jnp.tanh(0.5 * rounding_ref[row, col])
-            polarity = jnp.clip(full, -1.0, 1.0)
-            square = polarity * polarity
-            slope = jnp.where(square < 1.0, 0.3 - (0.3 / 1.44) * square, 0.0)
-            grad = slope * (scale * product[row, col] - (8.0 * reg_weight) * (square * polarity))
+            half = jnp.clip(0.6 * jnp.tanh(0.5 * rounding_ref[row, col]), -0.5, 0.5)
+            square = half * half
+            slope = jnp.where(square < 0.25, 0.36 - square, 0.0)
+            grad = slope * (scale * product[row, col] - square * half)
             grad_ref[row, col] = grad.astype(grad_ref.dtype)
             fold = lambda v: v.reshape(strip_r // 8, 8, strip_c).sum(axis=0)
-            return sums[0] + fold(grad * grad), sums[1] + fold(1.0 - square * square)
+            return sums[0] + fold(grad * grad), sums[1] + fold(0.0625 - square * square)
 
         zero = jnp.zeros((8, strip_c), jnp.float32)
         grads, pens = lax.fori_loop(0, trow // strip_r, strip, (zero, zero))
@@ -384,23 +392,35 @@
             out_ref.at[token_rows(m), :], carried.at[m], carry_sem.at[m], carry_recv.at[m], section + 1, z, t
         )
 
-    def complete(m):
-        finish(m)
-        for hop in range(min(dp, m + 1)):
-            gather_step(m - hop, hop)
-
-    for m in range(micro):
-        receive_rows(m)
-        rows_store(m).start()
-        multiply(m)
+    eager = section >= sections - 2
+
+    def gather(now):
+        for hop in range(dp):
+            if 0 <= now - LAG * hop < micro:
+                gather_step(now - LAG * hop, hop)
+
+    for m in range(micro + 1):
+        if m < micro:
+            receive_rows(m)
+            rows_store(m).start()
+            multiply(m)
         if m:
-            complete(m - 1)
-        combine(m)
-    complete(micro - 1)
-    for late in range(micro, micro + dp - 1):
-        for hop in range(dp):
-            if 0 <= late - hop < micro:
-                gather_step(late - hop, hop)
+            finish(m - 1)
+        if m < micro:
+            combine(m)
+        if m:
+
+            @pl.when(eager)
+            def _():
+                gather(m - 1)
+
+    @pl.when(jnp.logical_not(eager))
+    def _():
+        for now in range(micro):
+            gather(now)
+
+    for now in range(micro, micro + LAG * (dp - 1)):
+        gather(now)
     delta_store = pltpu.make_async_copy(delta, delta_hbm, store_sem.at[micro])
     delta_store.start()
 
@@ -525,6 +545,14 @@
             device_id={"dp": peer // nt, "tensor": lax.rem(peer, nt)}, device_id_type=pl.DeviceIdType.MESH,
         )
 
+    barrier = pltpu.get_barrier_semaphore()
+    for k in range(1, count):
+        peer = lax.rem(place + k, count)
+        pl.semaphore_signal(
+            barrier, inc=1, device_id={"dp": peer // nt, "tensor": lax.rem(peer, nt)},
+            device_id_type=pl.DeviceIdType.MESH,
+        )
+    pl.semaphore_wait(barrier, count - 1)
     for k in range(1, count):
         copy(k).start()
     held[place] = mine_ref[...]
@@ -555,7 +583,7 @@
             pltpu.SemaphoreType.DMA((count,)),
             pltpu.SemaphoreType.DMA((count,)),
         ],
-        compiler_params=pltpu.CompilerParams(has_side_effects=True),
+        compiler_params=pltpu.CompilerParams(has_side_effects=True, collective_id=0),
     )(mine)[:, 0, 0]
 
 
@@ -637,8 +665,9 @@
         recon_sum, penalty_sum, square_sum = lax.psum(
             (jnp.sum(residues), jnp.sum(sums[1]), jnp.sum(sums[0])), ("dp", "tensor")
         )
+    square_sum, penalty_sum = 256.0 * square_sum, 16.0 * penalty_sum
     mean_grad = square_sum / (width_full * width_full) + grad_eps
-    rounding_next = rounding[0] - step_rate * grad.astype(jnp.float32) * lax.rsqrt(mean_grad)
+    rounding_next = rounding[0] - (16.0 * step_rate) * grad.astype(jnp.float32) * lax.rsqrt(mean_grad)
     loss_value = recon_sum / (token_total * width_full) + reg_weight * penalty_sum / (
         width_full * width_full
     )

time: 410 us -> 377 us (0.920)
  Pallas kernels: 369 us -> 337 us
    pallas_call x1, Pallas kernels: 277 us -> 260 us  [run_chain(): pl.pallas_call(chain_kernel, out_shape=(jax.ShapeDtypeStruct((tok_dev, co...]
    pallas_call x1, Pallas kernels: 48.7 us -> 39.6 us  [make_grad(): pl.pallas_call(grad_kernel, out_shape=(jax.ShapeDtypeStruct((rows, cols),...]
where the time goes in v3:
time: 377 us; the launch traced here: 376 us
  Pallas kernels  337 us (89%)
  other arithmetic  29.6 us (8%)
  between operations  3.82 us (1%)
    pallas_call x1, Pallas kernels, run_chain(): pl.pallas_call(chain_kernel, out_shape=(jax.ShapeDtypeStruct((tok_dev, co...  260 us
    pallas_call x1, Pallas kernels, make_grad(): pl.pallas_call(grad_kernel, out_shape=(jax.ShapeDtypeStruct((rows, cols),...  39.6 us
    pallas_call x1, Pallas kernels, make_weight(): pl.pallas_call(weight_kernel, out_shape=jax.ShapeDtypeStruct((rows, cols)...  28.8 us
    broadcast_in_dim x1, other arithmetic, per_device(): return (rounding_next[None], outputs_buf[None], loss_value.reshape(1))  27.4 us
    pallas_call x1, Pallas kernels, add_sums(): pl.pallas_call(sums_kernel, out_shape=jax.ShapeDtypeStruct(mine.shape, mi...  7.97 us
  transfers between devices with their start and end apart: 1, of which 0 were waited for; matrix products, arithmetic and copies ran while one was open for 0% of the time, Pallas kernels for 8%

profile of v3, /device:TPU:7, one launch (start us, length us, event | category | flops | bytes accessed | tf_op | source)
XLA Modules:
  0.0 375.7 jit_solution(11937806836594003286)
XLA Ops:
  0.6 0.0 copy-start
  0.7 0.7 copy-done
  1.4 0.0 copy-start.3
  1.4 2.1 collective-permute-start
  3.6 28.8 %shard_map.85.weight_hbm = bf16[2048,4096]{1,0:T(8,128)(2,1)} custom-call(s32[512,4096]{1,0:T(8,128)} %bitcast.16, f32[2048,4096]{1,0:T(8,128)} %bitcast.14, f32[1,4096]{1,0:T(1,128)} %scale_ref.3), custom_call_target="tpu_custom_call" | custom-call | flops 167772160 | bytes 58720256 | tf_op jit(solution)/shard_map/pallas_call | solution.py:63
  32.4 0.0 collective-permute-done.gain_next_ref
  32.4 0.0 copy-start.4
  32.4 0.0 copy-done.3
  32.4 0.6 copy-done.4
  33.0 260.3 %shard_map.86 = (bf16[128,4096]{1,0:T(8,128)(2,1)}, f32[128,128]{1,0:T(8,128)}, bf16[8,4,16,2048]{3,2,1,0:T(8,128)(2,1)}, bf16[8,4,16,4096]{3,2,1,0:T(8,128)(2,1)}) custom-call(bf16[128,4096]{1,0:T(8,128)(2,1)} %act_ref.1, bf16[128,4096]{1,0:T(8,128)(2,1)} %bitcast.21, bf16[2048,4096]{1,0:T(8,128)(2,1)} %shard_map.85.weight_hbm, f32[1,4096]{1,0:T(1,128)} %copy-done.3, ...), custom_call_target="tpu_custom_call" | custom-call | flops 8589934592 | bytes 16777216 | tf_op jit(solution)/shard_map/pallas_call | solution.py:487
  293.2 0.9 bitcast_reduce_fusion
  294.1 39.6 %shard_map.87 = (bf16[2048,4096]{1,0:T(8,128)(2,1)}, f32[2,8,128]{2,1,0:T(8,128)}) custom-call(bf16[512,2048]{1,0:T(8,128)(2,1)} %bitcast.18, bf16[512,4096]{1,0:T(8,128)(2,1)} %bitcast.17, f32[2048,4096]{1,0:T(8,128)} %bitcast.15, f32[1,4096]{1,0:T(1,128)} %scale_ref.3), custom_call_target="tpu_custom_call" | custom-call | flops 8589934592 | bytes 50331648 | tf_op jit(solution)/shard_map/pallas_call | solution.py:120
  333.7 1.3 pad_maximum_fusion.mine_ref
  335.0 8.0 %shard_map.88 = f32[3,8,128]{2,1,0:T(8,128)} custom-call(f32[3,8,128]{2,1,0:T(8,128)} %pad_maximum_fusion.mine_ref), custom_call_target="tpu_custom_call" | custom-call | tf_op jit(solution)/shard_map/pallas_call | solution.py:576
  343.0 1.2 fusion
  346.2 0.0 copy-start.1
  346.2 0.0 copy-start.2
  346.2 27.4 %subtract_bitcast_fusion = f32[1,2048,4096]{2,1,0:T(8,128)} fusion(bf16[2048,4096]{1,0:T(8,128)(2,1)} %get-tuple-element.11, f32[]{:T(128)} %bitcast.7, f32[1,2048,4096]{2,1,0:T(8,128)} %param.9), kind=kLoop, calls=%fused_computation | loop fusion | flops 25165824 | bytes 83886080 | tf_op jit(solution)/shard_map/broadcast_in_dim | solution.py:674
  373.6 0.0 copy-done.2
  373.6 1.0 copy.10
  374.6 0.0 copy-done.1
  (2 shorter events, 0.0 us)
Async XLA Ops:
  0.6 0.8 copy-start
  1.4 31.0 %copy-start.3 = (f32[1,4096]{1,0:T(1,128)}, f32[1,4096]{1,0:T(1,128)S(1)}, u32[]{:S(2)}) copy-start(f32[1,4096]{1,0:T(1,128)S(1)} %constant_dynamic-slice_fusion.gain_ref) | copy-start | bytes 49156
  1.4 31.0 %collective-permute-start = (f32[1,4096]{1,0:T(1,128)S(1)}, f32[1,4096]{1,0:T(1,128)S(1)}, u32[]{:S(2)}, u32[]{:S(2)}) collective-permute-start(f32[1,4096]{1,0:T(1,128)S(1)} %constant_dynamic-slice_fusion.gain_ref), channel_id=1, source_target_pairs={{8,0},{16,8},{24,16},{9,1},{17,9},{25,17},{10,2},{18,10},{26,18},{... | collective-permute-start | bytes 49160 | tf_op jit(solution)/shard_map/ppermute | solution.py:593
  32.4 0.6 copy-start.4
  346.2 28.4 %copy-start.1 = (f32[1,8192]{1,0:T(1,128)S(1)}, f32[1,8192]{1,0:T(1,128)}, u32[]{:S(2)}) copy-start(f32[1,8192]{1,0:T(1,128)} %param.11) | copy-start | bytes 98308
  346.2 27.4 %copy-start.2 = (bf16[128,4096]{1,0:T(8,128)(2,1)S(1)}, bf16[128,4096]{1,0:T(8,128)(2,1)}, u32[]{:S(2)}) copy-start(bf16[128,4096]{1,0:T(8,128)(2,1)} %get-tuple-element.14) | copy-start | bytes 3145732
